TPU v7x, 32 devices: a whole 2x2x4 slice. The times are simulated.
32 devices in a mesh: groups: 2 (over x), seq: 16 (over z, y, core).
Axes of the slice: x: 2, y: 2, z: 4, core: 2. Of those that a mesh axis runs over, the one named last changes fastest.
Arguments:
- prefill_keys: bfloat16 [128, 4096, 128], P(('groups', 'seq')), parts along dimension 0, may hold values from -4 to 4
- prefill_values: bfloat16 [128, 4096, 128], P(('groups', 'seq')), parts along dimension 0, may hold values from -6 to 6
- window_queries: bfloat16 [128, 8, 256, 128], P(('groups', 'seq')), parts along dimension 0, may hold values from -48 to 48
- step_queries: bfloat16 [128, 2, 8, 128], P('groups'), parts along dimension 0, may hold values from -48 to 48
- new_keys: bfloat16 [128, 2, 128], P('groups'), parts along dimension 0, may hold values from -24 to 24
- new_values: bfloat16 [128, 2, 128], P('groups'), parts along dimension 0, may hold values from -6 to 6
- lengths: int32 [16], P('groups'), parts along dimension 0, may hold values from 2048 to 4096
- keep_mask: int32 [16, 32], P('groups'), parts along dimension 0, may hold values from 0 to 1, as said below
Outputs:
- cache_keys: bfloat16 [128, 4096, 128], P('groups', 'seq'), parts along dimension 0
- cache_values: bfloat16 [128, 4096, 128], P('groups', 'seq'), parts along dimension 0
- attended: bfloat16 [128, 2, 8, 128], P('groups'), parts along dimension 0
- block_scores: float32 [128, 32], P('groups', 'seq'), parts along dimension 0
There are 2 independent parts, one for each index of `groups`. A program takes and returns all parts, laid end to end along the dimension named above; each array names one. Nothing has to cross between parts.
Inputs may be any that keep to these rules, and one draw needn't show every extreme that they name: `keep_mask`: 1 keeps a block, 0 drops it; block 0 of every sequence is kept.
All inputs are finite; a program needn't handle non-finite values.
Results may differ from a plain program's by a relative error of at most 0.0055.
Values may be sent and summed in bfloat16 or wider, within the bound.
No kernel may reach another device: no remote copies, remote signals or barrier semaphores. Data moves between devices by JAX's collectives and lax.ppermute only.
A program may use at most 128 MiB of HBM per device.

v0:
```python
import math
import jax
import jax.numpy as jnp
from jax import lax
from jax.sharding import PartitionSpec as P

KVH = 8
GROUP = 8
BLOCK = 128


def window_mass(prefill_keys, window_queries, lengths, keep_mask, first_pair):
    pair_count, token_count, head_width = prefill_keys.shape
    block_count = keep_mask.shape[1]
    window_size = window_queries.shape[2]
    rows_pair = window_queries.shape[1] * window_size
    rows_block = math.gcd(rows_pair, 512)
    per_pair = rows_pair // rows_block
    flat_rows = window_queries.reshape(pair_count * per_pair, rows_block, head_width)
    scaling = 1.0 / math.sqrt(head_width)
    position = jnp.arange(token_count, dtype=jnp.int32)

    def one_block(block_index):
        pair_local = block_index // per_pair
        seq_id = (first_pair + pair_local) // KVH
        scores = (
            lax.dot_general(
                flat_rows[block_index],
                prefill_keys[pair_local],
                (((1,), (1,)), ((), ())),
                preferred_element_type=jnp.float32,
            )
            * scaling
        )
        row_offset = block_index % per_pair * rows_block + jnp.arange(rows_block, dtype=jnp.int32)
        query_pos = lengths[seq_id] - window_size + row_offset % window_size
        kept_tokens = jnp.broadcast_to(
            keep_mask[seq_id][:, None] > 0, (block_count, BLOCK)
        ).reshape(token_count)
        visible = kept_tokens[None, :] & (position[None, :] <= query_pos[:, None])
        scores = jnp.where(visible, scores, -jnp.inf)
        highest = jnp.max(scores, axis=1, keepdims=True)
        weights = jnp.exp(scores - highest)
        probability = weights / jnp.sum(weights, axis=1, keepdims=True)
        return jnp.sum(probability, axis=0).reshape(block_count, BLOCK).sum(axis=1)

    block_parts = lax.map(one_block, jnp.arange(pair_count * per_pair, dtype=jnp.int32))
    return block_parts.reshape(pair_count, per_pair, block_count).sum(axis=1) / GROUP


def select_rows(small_table, seq_ids):
    matches = seq_ids[:, None] == jnp.arange(small_table.shape[0], dtype=jnp.int32)[None, :]
    return jnp.sum(jnp.where(matches[:, :, None], small_table[None, :, :], 0), axis=1)


def step_scores(cache_part, queries_here, new_here, lengths, keep_mask, first_pair):
    pair_count, token_count, head_width = cache_part.shape
    step_count = queries_here.shape[1]
    group_size = queries_here.shape[2]
    query_rows = queries_here.reshape(pair_count, step_count * group_size, head_width)
    scaling = 1.0 / math.sqrt(head_width)
    scores = (
        jnp.einsum("pqd,ptd->pqt", query_rows, cache_part, preferred_element_type=jnp.float32)
        * scaling
    )
    seq_ids = (first_pair + jnp.arange(pair_count, dtype=jnp.int32)) // KVH
    block_count = token_count // BLOCK
    kept_blocks = select_rows(keep_mask, seq_ids) > 0
    kept_tokens = jnp.broadcast_to(
        kept_blocks[:, :, None], (pair_count, block_count, BLOCK)
    ).reshape(pair_count, token_count)
    seq_length = select_rows(lengths[:, None], seq_ids)[:, 0]
    position = jnp.arange(token_count, dtype=jnp.int32)
    visible = kept_tokens & (position[None, :] < seq_length[:, None])
    scores = jnp.where(visible[:, None, :], scores, -jnp.inf)
    own_scores = (
        jnp.einsum("pqd,pjd->pqj", query_rows, new_here, preferred_element_type=jnp.float32)
        * scaling
    )
    row_step = jnp.arange(step_count * group_size, dtype=jnp.int32) // group_size
    own_visible = jnp.arange(step_count, dtype=jnp.int32)[None, :] <= row_step[:, None]
    own_scores = jnp.where(own_visible[None], own_scores, -jnp.inf)
    return (scores, own_scores)


def local_terms(scores, cache_vals, highest):
    weights = jnp.exp(scores - highest[:, :, None])
    total_mass = jnp.sum(weights, axis=2)
    summed = jnp.einsum(
        "pqt,ptd->pqd", weights.astype(jnp.bfloat16), cache_vals, preferred_element_type=jnp.float32
    )
    return (weights, total_mass, summed)


def finish(summed, total_mass, weights, highest, own_scores, new_vals):
    own_weights = jnp.exp(own_scores - highest[:, :, None])
    total_mass = total_mass + jnp.sum(own_weights, axis=2)
    summed = summed + jnp.einsum(
        "pqj,pjd->pqd",
        own_weights.astype(jnp.bfloat16),
        new_vals,
        preferred_element_type=jnp.float32,
    )
    pair_count, row_count, head_width = summed.shape
    attended = (
        (summed / total_mass[:, :, None])
        .astype(jnp.bfloat16)
        .reshape(pair_count, row_count // GROUP, GROUP, head_width)
    )
    token_count = weights.shape[2]
    new_mass = (
        jnp.sum(weights / total_mass[:, :, None], axis=1)
        .reshape(pair_count, token_count // BLOCK, BLOCK)
        .sum(axis=2)
        / GROUP
    )
    return (attended, new_mass)


def local(
    prefill_keys,
    prefill_values,
    window_queries,
    step_queries,
    new_keys,
    new_values,
    lengths,
    keep_mask,
):
    pair_count = prefill_keys.shape[0]
    first_pair = lax.axis_index("seq") * pair_count
    prior_mass = window_mass(prefill_keys, window_queries, lengths, keep_mask, first_pair).astype(
        jnp.bfloat16
    )
    cache_keys, cache_values, prior_tokens = (
        lax.all_to_all(prefill_keys, "seq", split_axis=1, concat_axis=0, tiled=True),
        lax.all_to_all(prefill_values, "seq", split_axis=1, concat_axis=0, tiled=True),
        lax.all_to_all(prior_mass, "seq", split_axis=1, concat_axis=0, tiled=True),
    )
    queries_here = lax.dynamic_slice_in_dim(step_queries, first_pair, pair_count, 0)
    new_keys_here = lax.dynamic_slice_in_dim(new_keys, first_pair, pair_count, 0)
    new_values_here = lax.dynamic_slice_in_dim(new_values, first_pair, pair_count, 0)
    scores, own_scores = step_scores(
        prefill_keys, queries_here, new_keys_here, lengths, keep_mask, first_pair
    )
    highest = jnp.maximum(jnp.max(scores, axis=2), jnp.max(own_scores, axis=2))
    weights, total_mass, summed = local_terms(scores, prefill_values, highest)
    attended_here, mass_here = finish(
        summed, total_mass, weights, highest, own_scores, new_values_here
    )
    attended = lax.all_gather(attended_here, "seq", axis=0, tiled=True)
    new_mass = lax.all_to_all(mass_here, "seq", split_axis=1, concat_axis=0, tiled=True)
    block_scores = prior_tokens.astype(jnp.float32) + new_mass
    return (cache_keys, cache_values, attended, block_scores)


def solution(mesh):
    placed = (
        P(("groups", "seq"), None, None),
        P(("groups", "seq"), None, None),
        P(("groups", "seq"), None, None, None),
        P("groups", None, None, None),
        P("groups", None, None),
        P("groups", None, None),
        P("groups"),
        P("groups", None),
    )
    return jax.shard_map(
        local,
        mesh=mesh,
        in_specs=placed,
        out_specs=(
            P("groups", "seq", None),
            P("groups", "seq", None),
            P("groups", None, None, None),
            P("groups", "seq"),
        ),
        check_vma=False,
    )
```

profile of v0, /device:TPU:11, one launch (start us, length us, event | category | flops | bytes accessed | tf_op | source)
XLA Modules:
  0.0 480.5 jit_solution(5911037382524738119)
XLA Ops:
  0.7 232.3 %while.14 = (s32[]{:T(128)}, f32[16,32]{1,0:T(8,128)S(1)}, s32[16]{0:T(128)S(1)}, s32[]{:T(128)}, s32[8,32]{1,0:T(8,128)}, /*index=5*/s32[8]{0:T(128)}, bf16[16,...) while((s32[]{:T(128)}, f32[16,32]{1,0:T(8,128)S(1)}, ...), condition=%wide.region_11.12_spmd.clone, body=%wide.region_6.11_spmd.clone.sunk | while | flops 557848064 | bytes 26402040 | solution.py:47
  7.9 4.0 fusion.44
  13.1 1.9 divide_reduce_fusion.3
  22.4 4.0 fusion.44
  27.7 1.9 divide_reduce_fusion.3
  36.9 4.0 fusion.44
  51.5 4.0 fusion.44
  66.0 4.0 fusion.44
  71.2 1.9 divide_reduce_fusion.3
  80.5 4.0 fusion.44
  95.0 4.0 fusion.44
  109.5 4.0 fusion.44
  124.0 4.0 fusion.44
  138.6 4.0 fusion.44
  153.1 4.0 fusion.44
  167.6 4.0 fusion.44
  182.1 4.0 fusion.44
  196.6 4.0 fusion.44
  211.1 4.0 fusion.44
  225.7 4.0 fusion.44
  233.7 6.5 %all-to-all-start.2 = ((bf16[4,16,2]{0,2,1:T(2,128)(2,1)}), bf16[4,16,2]{0,2,1:T(2,128)(2,1)S(1)}, u32[]{:S(2)}, u32[]{:S(2)}) async-start(bf16[4,16,2]{0,2,1:T(2,128)(2,1)} %bitcast.10), calls=%async_computation.2 | async-start | bytes 16384 | tf_op jit(solution)/shard_map/all_to_all | solution.py:138
  242.1 3.5 fusion.36
  247.9 6.0 %all-to-all-start.3 = ((f32[4,16,2]{0,2,1:T(2,128)}), f32[4,16,2]{0,2,1:T(2,128)S(1)}, u32[]{:S(2)}, u32[]{:S(2)}) async-start(f32[4,16,2]{0,2,1:T(2,128)} %bitcast.11), calls=%async_computation.3 | async-start | bytes 32768 | tf_op jit(solution)/shard_map/all_to_all | solution.py:152
  253.9 7.6 %copy.27 = bf16[4,4096,128]{2,0,1:T(4,128)(2,1)} copy(bf16[4,4096,128]{2,1,0:T(8,128)(2,1)} %param.11) | data formatting | bytes 8388608 | tf_op args[1]
  261.5 6.0 %all-to-all-start.1 = ((bf16[4,4096,128]{2,0,1:T(4,128)(2,1)}), bf16[4,4096,128]{2,0,1:T(4,128)(2,1)}, u32[]{:S(2)}, u32[]{:S(2)}) async-start(bf16[4,4096,128]{2,0,1:T(4,128)(2,1)} %copy.27), calls=%async_computation.1 | async-start | bytes 8388608 | tf_op jit(solution)/shard_map/all_to_all | solution.py:137
  267.5 7.6 %copy.25 = bf16[4,4096,128]{2,0,1:T(4,128)(2,1)} copy(bf16[4,4096,128]{2,1,0:T(8,128)(2,1)} %get-tuple-element.321) | data formatting | bytes 8388608 | tf_op args[0]
  275.1 82.7 %all-to-all-done.1 = bf16[4,4096,128]{2,0,1:T(4,128)(2,1)} async-done(((bf16[4,4096,128]{2,0,1:T(4,128)(2,1)}), bf16[4,4096,128]{2,0,1:T(4,128)(2,1)}, u32[]{:S(2)}, u32[]{:S(2)}) %all-to-all-start.1) | async-done | bytes 4194336 | tf_op jit(solution)/shard_map/all_to_all | solution.py:137
  357.7 7.0 %all-to-all-start = ((bf16[4,4096,128]{2,0,1:T(4,128)(2,1)}), bf16[4,4096,128]{2,0,1:T(4,128)(2,1)}, u32[]{:S(2)}, u32[]{:S(2)}) async-start(bf16[4,4096,128]{2,0,1:T(4,128)(2,1)} %copy.25), calls=%async_computation | async-start | bytes 8388608 | tf_op jit(solution)/shard_map/all_to_all | solution.py:136
  364.8 2.9 fusion.18
  368.6 99.9 %all_gather.3 = bf16[64,2,8,128]{3,2,1,0:T(8,128)(2,1)S(1)} all-gather(bf16[4,2,8,128]{3,2,1,0:T(8,128)(2,1)S(1)} %fusion.14), channel_id=1, replica_groups=mesh['groups'=2,'seq'=16] {'seq'}, dimensions={0}, use_global_device_ids=true | all-gather | bytes 278528 | tf_op jit(solution)/shard_map/all_gather | solution.py:151
  469.1 5.3 %copy.28 = bf16[16,4,256,128]{3,2,1,0:T(8,128)(2,1)} copy(bf16[16,4,256,128]{3,1,2,0:T(4,128)(2,1)} %bitcast.4) | data formatting | bytes 8388608 | tf_op jit(solution)/shard_map/all_to_all | solution.py:137
  474.5 5.3 %copy.26 = bf16[16,4,256,128]{3,2,1,0:T(8,128)(2,1)} copy(bf16[16,4,256,128]{3,1,2,0:T(4,128)(2,1)} %bitcast.1) | data formatting | bytes 8388608 | tf_op jit(solution)/shard_map/all_to_all | solution.py:136
  (174 shorter events, 96.5 us)
Async XLA Ops:
  0.6 241.4 %copy-start = (bf16[64,2,8,128]{3,2,1,0:T(8,128)(2,1)S(1)}, bf16[64,2,8,128]{3,2,1,0:T(8,128)(2,1)}, u32[]{:S(2)}) copy-start(bf16[64,2,8,128]{3,2,1,0:T(8,128)(2,1)} %param.13) | copy-start | bytes 786436
  233.7 14.2 %all-to-all-start.2 = ((bf16[4,16,2]{0,2,1:T(2,128)(2,1)}), bf16[4,16,2]{0,2,1:T(2,128)(2,1)S(1)}, u32[]{:S(2)}, u32[]{:S(2)}) async-start(bf16[4,16,2]{0,2,1:T(2,128)(2,1)} %bitcast.10), calls=%async_computation.2 | async-start | bytes 16384 | tf_op jit(solution)/shard_map/all_to_all | solution.py:138
  247.9 13.6 %all-to-all-start.3 = ((f32[4,16,2]{0,2,1:T(2,128)}), f32[4,16,2]{0,2,1:T(2,128)S(1)}, u32[]{:S(2)}, u32[]{:S(2)}) async-start(f32[4,16,2]{0,2,1:T(2,128)} %bitcast.11), calls=%async_computation.3 | async-start | bytes 32768 | tf_op jit(solution)/shard_map/all_to_all | solution.py:152
  261.5 96.2 %all-to-all-start.1 = ((bf16[4,4096,128]{2,0,1:T(4,128)(2,1)}), bf16[4,4096,128]{2,0,1:T(4,128)(2,1)}, u32[]{:S(2)}, u32[]{:S(2)}) async-start(bf16[4,4096,128]{2,0,1:T(4,128)(2,1)} %copy.27), calls=%async_computation.1 | async-start | bytes 8388608 | tf_op jit(solution)/shard_map/all_to_all | solution.py:137
  357.7 116.7 %all-to-all-start = ((bf16[4,4096,128]{2,0,1:T(4,128)(2,1)}), bf16[4,4096,128]{2,0,1:T(4,128)(2,1)}, u32[]{:S(2)}, u32[]{:S(2)}) async-start(bf16[4,4096,128]{2,0,1:T(4,128)(2,1)} %copy.25), calls=%async_computation | async-start | bytes 8388608 | tf_op jit(solution)/shard_map/all_to_all | solution.py:136
where the time goes:
time: 483 us; the launch traced here: 481 us
  blocking collectives  99.9 us (21%)
  waiting for transfers between devices  82.7 us (17%)
  loops' own time  73.9 us (15%)
  matrix products  71.5 us (15%)
  other arithmetic  66.7 us (14%)
  local copies, waits for them, and re-layouts  59.6 us (12%)
  starting transfers between devices  25.5 us (5%)
    all_gather x1, blocking collectives, local(): attended = lax.all_gather(attended_here, 'seq', axis=0, tiled=True)  99.9 us
    all_to_all x1, waiting for transfers between devices, local(): lax.all_to_all(prefill_values, 'seq', split_axis=1, concat_axis=0, tiled=...  82.7 us
    another operation x1, loops' own time, window_mass(): lax.map(one_block, jnp.arange(pair_count * per_pair, dtype=jnp.int32))  73.9 us
    dot_general x16, matrix products, one_block(): lax.dot_general(flat_rows[block_index], prefill_keys[pair_local], (((1,),...  63.4 us
    reduce_sum x32, other arithmetic, one_block(): return jnp.sum(probability, axis=0).reshape(block_count, BLOCK).sum(axis=1)  32.1 us
    reduce_sum x16, other arithmetic, one_block(): probability = weights / jnp.sum(weights, axis=1, keepdims=True)  20.6 us
    dynamic_slice x16, local copies, waits for them, and re-layouts, one_block(): query_pos = lengths[seq_id] - window_size + row_offset % window_size  19.9 us
    unnamed x6, local copies, waits for them, and re-layouts  15.9 us
  transfers between devices with their start and end apart: 4, of which 1 were waited for; matrix products, arithmetic and copies ran while one was open for 7% of the time, Pallas kernels for 0%

commit v1 on v0

--- a/solution.py
+++ b/solution.py
@@ -148,7 +148,13 @@
     attended_here, mass_here = finish(
         summed, total_mass, weights, highest, own_scores, new_values_here
     )
-    attended = lax.all_gather(attended_here, "seq", axis=0, tiled=True)
+    size = lax.axis_size("seq")
+    held, shards = (attended_here, [attended_here])
+    for _ in range(size - 1):
+        held = lax.ppermute(held, "seq", [(i, (i + 1) % size) for i in range(size)])
+        shards.insert(0, held)
+    flat = jnp.concatenate(shards, axis=0)
+    attended = jnp.roll(flat, (lax.axis_index("seq") + 1) * attended_here.shape[0], axis=0)
     new_mass = lax.all_to_all(mass_here, "seq", split_axis=1, concat_axis=0, tiled=True)
     block_scores = prior_tokens.astype(jnp.float32) + new_mass
     return (cache_keys, cache_values, attended, block_scores)

time: 483 us -> 536 us (1.11)
  the two profiles are of different devices: /device:TPU:11 before, /device:TPU:0 now
where the time goes in v1:
time: 536 us; the launch traced here: 533 us
  waiting for transfers between devices  221 us (41%)
  loops' own time  73.9 us (14%)
  matrix products  71.4 us (13%)
  other arithmetic  66.7 us (12%)
  local copies, waits for them, and re-layouts  59.9 us (11%)
  starting transfers between devices  39.6 us (7%)
    ppermute x15, waiting for transfers between devices, local(): held = lax.ppermute(held, 'seq', [(i, (i + 1) % size) for i in range(size)])  151 us
    another operation x1, loops' own time, window_mass(): lax.map(one_block, jnp.arange(pair_count * per_pair, dtype=jnp.int32))  73.9 us
    all_to_all x1, waiting for transfers between devices, local(): lax.all_to_all(prefill_values, 'seq', split_axis=1, concat_axis=0, tiled=...  70 us
    dot_general x16, matrix products, one_block(): lax.dot_general(flat_rows[block_index], prefill_keys[pair_local], (((1,),...  63.3 us
    reduce_sum x32, other arithmetic, one_block(): return jnp.sum(probability, axis=0).reshape(block_count, BLOCK).sum(axis=1)  32.1 us
    reduce_sum x16, other arithmetic, one_block(): probability = weights / jnp.sum(weights, axis=1, keepdims=True)  20.6 us
    dynamic_slice x16, local copies, waits for them, and re-layouts, one_block(): query_pos = lengths[seq_id] - window_size + row_offset % window_size  19.9 us
    all_to_all x1, starting transfers between devices, local(): lax.all_to_all(prefill_keys, 'seq', split_axis=1, concat_axis=0, tiled=True)  19.7 us
  transfers between devices with their start and end apart: 19, of which 16 were waited for; matrix products, arithmetic and copies ran while one was open for 6% of the time, Pallas kernels for 0%

profile of v1, /device:TPU:0, one launch (start us, length us, event | category | flops | bytes accessed | tf_op | source)
XLA Modules:
  0.0 533.1 jit_solution(14871432760783443629)
XLA Ops:
  0.7 232.2 %while.14 = (s32[]{:T(128)}, f32[16,32]{1,0:T(8,128)S(1)}, s32[16]{0:T(128)S(1)}, s32[]{:T(128)}, s32[8,32]{1,0:T(8,128)}, /*index=5*/s32[8]{0:T(128)}, bf16[16,...) while((s32[]{:T(128)}, f32[16,32]{1,0:T(8,128)S(1)}, ...), condition=%wide.region_11.12_spmd.clone, body=%wide.region_6.11_spmd.clone.sunk | while | flops 557848064 | bytes 26402040 | solution.py:47
  7.9 4.0 fusion.44
  36.9 4.0 fusion.44
  51.4 4.0 fusion.44
  94.9 4.0 fusion.44
  138.5 4.0 fusion.44
  182.0 4.0 fusion.44
  225.5 4.0 fusion.44
  233.6 7.4 %all-to-all-start.2 = ((bf16[4,16,2]{0,2,1:T(2,128)(2,1)}), bf16[4,16,2]{0,2,1:T(2,128)(2,1)S(1)}, u32[]{:S(2)}, u32[]{:S(2)}) async-start(bf16[4,16,2]{0,2,1:T(2,128)(2,1)} %bitcast.10), calls=%async_computation.2 | async-start | bytes 16384 | tf_op jit(solution)/shard_map/all_to_all | solution.py:138
  248.7 6.0 %all-to-all-start.3 = ((f32[4,16,2]{0,2,1:T(2,128)}), f32[4,16,2]{0,2,1:T(2,128)S(1)}, u32[]{:S(2)}, u32[]{:S(2)}) async-start(f32[4,16,2]{0,2,1:T(2,128)} %bitcast.11), calls=%async_computation.3 | async-start | bytes 32768 | tf_op jit(solution)/shard_map/all_to_all | solution.py:158
  254.8 7.6 %copy.27 = bf16[4,4096,128]{2,0,1:T(4,128)(2,1)} copy(bf16[4,4096,128]{2,1,0:T(8,128)(2,1)} %param.11) | data formatting | bytes 8388608 | tf_op args[1]
  262.3 6.1 %all-to-all-start.1 = ((bf16[4,4096,128]{2,0,1:T(4,128)(2,1)}), bf16[4,4096,128]{2,0,1:T(4,128)(2,1)}, u32[]{:S(2)}, u32[]{:S(2)}) async-start(bf16[4,4096,128]{2,0,1:T(4,128)(2,1)} %copy.27), calls=%async_computation.1 | async-start | bytes 8388608 | tf_op jit(solution)/shard_map/all_to_all | solution.py:137
  268.4 7.6 %copy.25 = bf16[4,4096,128]{2,0,1:T(4,128)(2,1)} copy(bf16[4,4096,128]{2,1,0:T(8,128)(2,1)} %get-tuple-element.313) | data formatting | bytes 8388608 | tf_op args[0]
  276.0 70.0 %all-to-all-done.1 = bf16[4,4096,128]{2,0,1:T(4,128)(2,1)} async-done(((bf16[4,4096,128]{2,0,1:T(4,128)(2,1)}), bf16[4,4096,128]{2,0,1:T(4,128)(2,1)}, u32[]{:S(2)}, u32[]{:S(2)}) %all-to-all-start.1) | async-done | bytes 4194336 | tf_op jit(solution)/shard_map/all_to_all | solution.py:137
  345.9 19.7 %all-to-all-start = ((bf16[4,4096,128]{2,0,1:T(4,128)(2,1)}), bf16[4,4096,128]{2,0,1:T(4,128)(2,1)}, u32[]{:S(2)}, u32[]{:S(2)}) async-start(bf16[4,4096,128]{2,0,1:T(4,128)(2,1)} %copy.25), calls=%async_computation | async-start | bytes 8388608 | tf_op jit(solution)/shard_map/all_to_all | solution.py:136
  369.9 69.1 %collective-permute-done = bf16[4,2,8,128]{3,2,1,0:T(8,128)(2,1)S(1)} collective-permute-done((bf16[4,2,8,128]{3,2,1,0:T(8,128)(2,1)S(1)}, bf16[4,2,8,128]{3,2,1,0:T(8,128)(2,1)S(1)}, u32[]{:S(2)}, u32[]{:S(2)}) %collective-permute-start) | collective-permute-done | bytes 16416 | tf_op jit(solution)/shard_map/ppermute | solution.py:154
  438.9 6.0 %collective-permute-done.1 = bf16[4,2,8,128]{3,2,1,0:T(8,128)(2,1)S(1)} collective-permute-done((bf16[4,2,8,128]{3,2,1,0:T(8,128)(2,1)S(1)}, bf16[4,2,8,128]{3,2,1,0:T(8,128)(2,1)S(1)}, u32[]{:S(2)}, u32[]{:S(2)}) %collective-permute-start.1) | collective-permute-done | bytes 16416 | tf_op jit(solution)/shard_map/ppermute | solution.py:154
  444.9 6.0 %collective-permute-done.2 = bf16[4,2,8,128]{3,2,1,0:T(8,128)(2,1)S(1)} collective-permute-done((bf16[4,2,8,128]{3,2,1,0:T(8,128)(2,1)S(1)}, bf16[4,2,8,128]{3,2,1,0:T(8,128)(2,1)S(1)}, u32[]{:S(2)}, u32[]{:S(2)}) %collective-permute-start.2) | collective-permute-done | bytes 16416 | tf_op jit(solution)/shard_map/ppermute | solution.py:154
  450.8 6.0 %collective-permute-done.3 = bf16[4,2,8,128]{3,2,1,0:T(8,128)(2,1)S(1)} collective-permute-done((bf16[4,2,8,128]{3,2,1,0:T(8,128)(2,1)S(1)}, bf16[4,2,8,128]{3,2,1,0:T(8,128)(2,1)S(1)}, u32[]{:S(2)}, u32[]{:S(2)}) %collective-permute-start.3) | collective-permute-done | bytes 16416 | tf_op jit(solution)/shard_map/ppermute | solution.py:154
  456.8 5.9 %collective-permute-done.4 = bf16[4,2,8,128]{3,2,1,0:T(8,128)(2,1)S(1)} collective-permute-done((bf16[4,2,8,128]{3,2,1,0:T(8,128)(2,1)S(1)}, bf16[4,2,8,128]{3,2,1,0:T(8,128)(2,1)S(1)}, u32[]{:S(2)}, u32[]{:S(2)}) %collective-permute-start.4) | collective-permute-done | bytes 16416 | tf_op jit(solution)/shard_map/ppermute | solution.py:154
  462.7 5.9 %collective-permute-done.5 = bf16[4,2,8,128]{3,2,1,0:T(8,128)(2,1)S(1)} collective-permute-done((bf16[4,2,8,128]{3,2,1,0:T(8,128)(2,1)S(1)}, bf16[4,2,8,128]{3,2,1,0:T(8,128)(2,1)S(1)}, u32[]{:S(2)}, u32[]{:S(2)}) %collective-permute-start.5) | collective-permute-done | bytes 16416 | tf_op jit(solution)/shard_map/ppermute | solution.py:154
  468.5 5.9 %collective-permute-done.6 = bf16[4,2,8,128]{3,2,1,0:T(8,128)(2,1)S(1)} collective-permute-done((bf16[4,2,8,128]{3,2,1,0:T(8,128)(2,1)S(1)}, bf16[4,2,8,128]{3,2,1,0:T(8,128)(2,1)S(1)}, u32[]{:S(2)}, u32[]{:S(2)}) %collective-permute-start.6) | collective-permute-done | bytes 16416 | tf_op jit(solution)/shard_map/ppermute | solution.py:154
  474.4 5.9 %collective-permute-done.7 = bf16[4,2,8,128]{3,2,1,0:T(8,128)(2,1)S(1)} collective-permute-done((bf16[4,2,8,128]{3,2,1,0:T(8,128)(2,1)S(1)}, bf16[4,2,8,128]{3,2,1,0:T(8,128)(2,1)S(1)}, u32[]{:S(2)}, u32[]{:S(2)}) %collective-permute-start.7) | collective-permute-done | bytes 16416 | tf_op jit(solution)/shard_map/ppermute | solution.py:154
  480.2 5.9 %collective-permute-done.8 = bf16[4,2,8,128]{3,2,1,0:T(8,128)(2,1)S(1)} collective-permute-done((bf16[4,2,8,128]{3,2,1,0:T(8,128)(2,1)S(1)}, bf16[4,2,8,128]{3,2,1,0:T(8,128)(2,1)S(1)}, u32[]{:S(2)}, u32[]{:S(2)}) %collective-permute-start.8) | collective-permute-done | bytes 16416 | tf_op jit(solution)/shard_map/ppermute | solution.py:154
  486.1 5.9 %collective-permute-done.9 = bf16[4,2,8,128]{3,2,1,0:T(8,128)(2,1)S(1)} collective-permute-done((bf16[4,2,8,128]{3,2,1,0:T(8,128)(2,1)S(1)}, bf16[4,2,8,128]{3,2,1,0:T(8,128)(2,1)S(1)}, u32[]{:S(2)}, u32[]{:S(2)}) %collective-permute-start.9) | collective-permute-done | bytes 16416 | tf_op jit(solution)/shard_map/ppermute | solution.py:154
  492.0 5.9 %collective-permute-done.10 = bf16[4,2,8,128]{3,2,1,0:T(8,128)(2,1)S(1)} collective-permute-done((bf16[4,2,8,128]{3,2,1,0:T(8,128)(2,1)S(1)}, bf16[4,2,8,128]{3,2,1,0:T(8,128)(2,1)S(1)}, u32[]{:S(2)}, u32[]{:S(2)}) %collective-permute-start.10) | collective-permute-done | bytes 16416 | tf_op jit(solution)/shard_map/ppermute | solution.py:154
  497.8 5.9 %collective-permute-done.11 = bf16[4,2,8,128]{3,2,1,0:T(8,128)(2,1)S(1)} collective-permute-done((bf16[4,2,8,128]{3,2,1,0:T(8,128)(2,1)S(1)}, bf16[4,2,8,128]{3,2,1,0:T(8,128)(2,1)S(1)}, u32[]{:S(2)}, u32[]{:S(2)}) %collective-permute-start.11) | collective-permute-done | bytes 16416 | tf_op jit(solution)/shard_map/ppermute | solution.py:154
  503.7 5.9 %collective-permute-done.12 = bf16[4,2,8,128]{3,2,1,0:T(8,128)(2,1)S(1)} collective-permute-done((bf16[4,2,8,128]{3,2,1,0:T(8,128)(2,1)S(1)}, bf16[4,2,8,128]{3,2,1,0:T(8,128)(2,1)S(1)}, u32[]{:S(2)}, u32[]{:S(2)}) %collective-permute-start.12) | collective-permute-done | bytes 16416 | tf_op jit(solution)/shard_map/ppermute | solution.py:154
  509.6 5.9 %collective-permute-done.13 = bf16[4,2,8,128]{3,2,1,0:T(8,128)(2,1)S(1)} collective-permute-done((bf16[4,2,8,128]{3,2,1,0:T(8,128)(2,1)S(1)}, bf16[4,2,8,128]{3,2,1,0:T(8,128)(2,1)S(1)}, u32[]{:S(2)}, u32[]{:S(2)}) %collective-permute-start.13) | collective-permute-done | bytes 16416 | tf_op jit(solution)/shard_map/ppermute | solution.py:154
  516.1 5.2 collective-permute-done.14
  522.4 5.3 %copy.28 = bf16[16,4,256,128]{3,2,1,0:T(8,128)(2,1)} copy(bf16[16,4,256,128]{3,1,2,0:T(4,128)(2,1)} %bitcast.4) | data formatting | bytes 8388608 | tf_op jit(solution)/shard_map/all_to_all | solution.py:137
  527.7 5.3 %copy.26 = bf16[16,4,256,128]{3,2,1,0:T(8,128)(2,1)} copy(bf16[16,4,256,128]{3,1,2,0:T(4,128)(2,1)} %bitcast.1) | data formatting | bytes 8388608 | tf_op jit(solution)/shard_map/all_to_all | solution.py:136
  (235 shorter events, 145.0 us)
Async XLA Ops:
  0.6 242.3 %copy-start = (bf16[64,2,8,128]{3,2,1,0:T(8,128)(2,1)S(1)}, bf16[64,2,8,128]{3,2,1,0:T(8,128)(2,1)}, u32[]{:S(2)}) copy-start(bf16[64,2,8,128]{3,2,1,0:T(8,128)(2,1)} %param.13) | copy-start | bytes 786436
  233.6 15.2 %all-to-all-start.2 = ((bf16[4,16,2]{0,2,1:T(2,128)(2,1)}), bf16[4,16,2]{0,2,1:T(2,128)(2,1)S(1)}, u32[]{:S(2)}, u32[]{:S(2)}) async-start(bf16[4,16,2]{0,2,1:T(2,128)(2,1)} %bitcast.10), calls=%async_computation.2 | async-start | bytes 16384 | tf_op jit(solution)/shard_map/all_to_all | solution.py:138
  248.7 13.6 %all-to-all-start.3 = ((f32[4,16,2]{0,2,1:T(2,128)}), f32[4,16,2]{0,2,1:T(2,128)S(1)}, u32[]{:S(2)}, u32[]{:S(2)}) async-start(f32[4,16,2]{0,2,1:T(2,128)} %bitcast.11), calls=%async_computation.3 | async-start | bytes 32768 | tf_op jit(solution)/shard_map/all_to_all | solution.py:158
  262.3 83.6 %all-to-all-start.1 = ((bf16[4,4096,128]{2,0,1:T(4,128)(2,1)}), bf16[4,4096,128]{2,0,1:T(4,128)(2,1)}, u32[]{:S(2)}, u32[]{:S(2)}) async-start(bf16[4,4096,128]{2,0,1:T(4,128)(2,1)} %copy.27), calls=%async_computation.1 | async-start | bytes 8388608 | tf_op jit(solution)/shard_map/all_to_all | solution.py:137
  345.9 181.8 %all-to-all-start = ((bf16[4,4096,128]{2,0,1:T(4,128)(2,1)}), bf16[4,4096,128]{2,0,1:T(4,128)(2,1)}, u32[]{:S(2)}, u32[]{:S(2)}) async-start(bf16[4,4096,128]{2,0,1:T(4,128)(2,1)} %copy.25), calls=%async_computation | async-start | bytes 8388608 | tf_op jit(solution)/shard_map/all_to_all | solution.py:136
  369.4 69.5 %collective-permute-start = (bf16[4,2,8,128]{3,2,1,0:T(8,128)(2,1)S(1)}, bf16[4,2,8,128]{3,2,1,0:T(8,128)(2,1)S(1)}, u32[]{:S(2)}, u32[]{:S(2)}) collective-permute-start(bf16[4,2,8,128]{3,2,1,0:T(8,128)(2,1)S(1)} %fusion.14), channel_id=1, source_target_pairs={{0,1},{1,2},{2,3},{3,4},{4,5},{5,6},{6,7},{7,8},{8,9},{9,10},{10,1... | collective-permute-start | bytes 49160 | tf_op jit(solution)/shard_map/ppermute | solution.py:154
  438.9 6.0 %collective-permute-start.1 = (bf16[4,2,8,128]{3,2,1,0:T(8,128)(2,1)S(1)}, bf16[4,2,8,128]{3,2,1,0:T(8,128)(2,1)S(1)}, u32[]{:S(2)}, u32[]{:S(2)}) collective-permute-start(bf16[4,2,8,128]{3,2,1,0:T(8,128)(2,1)S(1)} %collective-permute-done), channel_id=1, source_target_pairs={{0,1},{1,2},{2,3},{3,4},{4,5},{5,6},{6,7},{7,8},{8,9},{9,10},{10,1... | collective-permute-start | bytes 49160 | tf_op jit(solution)/shard_map/ppermute | solution.py:154
  444.9 6.0 %collective-permute-start.2 = (bf16[4,2,8,128]{3,2,1,0:T(8,128)(2,1)S(1)}, bf16[4,2,8,128]{3,2,1,0:T(8,128)(2,1)S(1)}, u32[]{:S(2)}, u32[]{:S(2)}) collective-permute-start(bf16[4,2,8,128]{3,2,1,0:T(8,128)(2,1)S(1)} %collective-permute-done.1), channel_id=1, source_target_pairs={{0,1},{1,2},{2,3},{3,4},{4,5},{5,6},{6,7},{7,8},{8,9},{9,10},{10,1... | collective-permute-start | bytes 49160 | tf_op jit(solution)/shard_map/ppermute | solution.py:154
  450.8 6.0 %collective-permute-start.3 = (bf16[4,2,8,128]{3,2,1,0:T(8,128)(2,1)S(1)}, bf16[4,2,8,128]{3,2,1,0:T(8,128)(2,1)S(1)}, u32[]{:S(2)}, u32[]{:S(2)}) collective-permute-start(bf16[4,2,8,128]{3,2,1,0:T(8,128)(2,1)S(1)} %collective-permute-done.2), channel_id=1, source_target_pairs={{0,1},{1,2},{2,3},{3,4},{4,5},{5,6},{6,7},{7,8},{8,9},{9,10},{10,1... | collective-permute-start | bytes 49160 | tf_op jit(solution)/shard_map/ppermute | solution.py:154
  456.8 5.9 %collective-permute-start.4 = (bf16[4,2,8,128]{3,2,1,0:T(8,128)(2,1)S(1)}, bf16[4,2,8,128]{3,2,1,0:T(8,128)(2,1)S(1)}, u32[]{:S(2)}, u32[]{:S(2)}) collective-permute-start(bf16[4,2,8,128]{3,2,1,0:T(8,128)(2,1)S(1)} %collective-permute-done.3), channel_id=1, source_target_pairs={{0,1},{1,2},{2,3},{3,4},{4,5},{5,6},{6,7},{7,8},{8,9},{9,10},{10,1... | collective-permute-start | bytes 49160 | tf_op jit(solution)/shard_map/ppermute | solution.py:154
  462.7 5.9 %collective-permute-start.5 = (bf16[4,2,8,128]{3,2,1,0:T(8,128)(2,1)S(1)}, bf16[4,2,8,128]{3,2,1,0:T(8,128)(2,1)S(1)}, u32[]{:S(2)}, u32[]{:S(2)}) collective-permute-start(bf16[4,2,8,128]{3,2,1,0:T(8,128)(2,1)S(1)} %collective-permute-done.4), channel_id=1, source_target_pairs={{0,1},{1,2},{2,3},{3,4},{4,5},{5,6},{6,7},{7,8},{8,9},{9,10},{10,1... | collective-permute-start | bytes 49160 | tf_op jit(solution)/shard_map/ppermute | solution.py:154
  468.5 5.9 %collective-permute-start.6 = (bf16[4,2,8,128]{3,2,1,0:T(8,128)(2,1)S(1)}, bf16[4,2,8,128]{3,2,1,0:T(8,128)(2,1)S(1)}, u32[]{:S(2)}, u32[]{:S(2)}) collective-permute-start(bf16[4,2,8,128]{3,2,1,0:T(8,128)(2,1)S(1)} %collective-permute-done.5), channel_id=1, source_target_pairs={{0,1},{1,2},{2,3},{3,4},{4,5},{5,6},{6,7},{7,8},{8,9},{9,10},{10,1... | collective-permute-start | bytes 49160 | tf_op jit(solution)/shard_map/ppermute | solution.py:154
  474.4 5.9 %collective-permute-start.7 = (bf16[4,2,8,128]{3,2,1,0:T(8,128)(2,1)S(1)}, bf16[4,2,8,128]{3,2,1,0:T(8,128)(2,1)S(1)}, u32[]{:S(2)}, u32[]{:S(2)}) collective-permute-start(bf16[4,2,8,128]{3,2,1,0:T(8,128)(2,1)S(1)} %collective-permute-done.6), channel_id=1, source_target_pairs={{0,1},{1,2},{2,3},{3,4},{4,5},{5,6},{6,7},{7,8},{8,9},{9,10},{10,1... | collective-permute-start | bytes 49160 | tf_op jit(solution)/shard_map/ppermute | solution.py:154
  480.2 5.9 %collective-permute-start.8 = (bf16[4,2,8,128]{3,2,1,0:T(8,128)(2,1)S(1)}, bf16[4,2,8,128]{3,2,1,0:T(8,128)(2,1)S(1)}, u32[]{:S(2)}, u32[]{:S(2)}) collective-permute-start(bf16[4,2,8,128]{3,2,1,0:T(8,128)(2,1)S(1)} %collective-permute-done.7), channel_id=1, source_target_pairs={{0,1},{1,2},{2,3},{3,4},{4,5},{5,6},{6,7},{7,8},{8,9},{9,10},{10,1... | collective-permute-start | bytes 49160 | tf_op jit(solution)/shard_map/ppermute | solution.py:154
  486.1 5.9 %collective-permute-start.9 = (bf16[4,2,8,128]{3,2,1,0:T(8,128)(2,1)S(1)}, bf16[4,2,8,128]{3,2,1,0:T(8,128)(2,1)S(1)}, u32[]{:S(2)}, u32[]{:S(2)}) collective-permute-start(bf16[4,2,8,128]{3,2,1,0:T(8,128)(2,1)S(1)} %collective-permute-done.8), channel_id=1, source_target_pairs={{0,1},{1,2},{2,3},{3,4},{4,5},{5,6},{6,7},{7,8},{8,9},{9,10},{10,1... | collective-permute-start | bytes 49160 | tf_op jit(solution)/shard_map/ppermute | solution.py:154
  492.0 5.9 %collective-permute-start.10 = (bf16[4,2,8,128]{3,2,1,0:T(8,128)(2,1)S(1)}, bf16[4,2,8,128]{3,2,1,0:T(8,128)(2,1)S(1)}, u32[]{:S(2)}, u32[]{:S(2)}) collective-permute-start(bf16[4,2,8,128]{3,2,1,0:T(8,128)(2,1)S(1)} %collective-permute-done.9), channel_id=1, source_target_pairs={{0,1},{1,2},{2,3},{3,4},{4,5},{5,6},{6,7},{7,8},{8,9},{9,10},{10,1... | collective-permute-start | bytes 49160 | tf_op jit(solution)/shard_map/ppermute | solution.py:154
  497.8 5.9 %collective-permute-start.11 = (bf16[4,2,8,128]{3,2,1,0:T(8,128)(2,1)S(1)}, bf16[4,2,8,128]{3,2,1,0:T(8,128)(2,1)S(1)}, u32[]{:S(2)}, u32[]{:S(2)}) collective-permute-start(bf16[4,2,8,128]{3,2,1,0:T(8,128)(2,1)S(1)} %collective-permute-done.10), channel_id=1, source_target_pairs={{0,1},{1,2},{2,3},{3,4},{4,5},{5,6},{6,7},{7,8},{8,9},{9,10},{10,1... | collective-permute-start | bytes 49160 | tf_op jit(solution)/shard_map/ppermute | solution.py:154
  503.7 5.9 %collective-permute-start.12 = (bf16[4,2,8,128]{3,2,1,0:T(8,128)(2,1)S(1)}, bf16[4,2,8,128]{3,2,1,0:T(8,128)(2,1)S(1)}, u32[]{:S(2)}, u32[]{:S(2)}) collective-permute-start(bf16[4,2,8,128]{3,2,1,0:T(8,128)(2,1)S(1)} %collective-permute-done.11), channel_id=1, source_target_pairs={{0,1},{1,2},{2,3},{3,4},{4,5},{5,6},{6,7},{7,8},{8,9},{9,10},{10,1... | collective-permute-start | bytes 49160 | tf_op jit(solution)/shard_map/ppermute | solution.py:154
  509.6 5.9 %collective-permute-start.13 = (bf16[4,2,8,128]{3,2,1,0:T(8,128)(2,1)S(1)}, bf16[4,2,8,128]{3,2,1,0:T(8,128)(2,1)S(1)}, u32[]{:S(2)}, u32[]{:S(2)}) collective-permute-start(bf16[4,2,8,128]{3,2,1,0:T(8,128)(2,1)S(1)} %collective-permute-done.12), channel_id=1, source_target_pairs={{0,1},{1,2},{2,3},{3,4},{4,5},{5,6},{6,7},{7,8},{8,9},{9,10},{10,1... | collective-permute-start | bytes 49160 | tf_op jit(solution)/shard_map/ppermute | solution.py:154
  515.4 5.9 %collective-permute-start.14 = (bf16[4,2,8,128]{3,2,1,0:T(8,128)(2,1)S(1)}, bf16[4,2,8,128]{3,2,1,0:T(8,128)(2,1)S(1)}, u32[]{:S(2)}, u32[]{:S(2)}) collective-permute-start(bf16[4,2,8,128]{3,2,1,0:T(8,128)(2,1)S(1)} %collective-permute-done.13), channel_id=1, source_target_pairs={{0,1},{1,2},{2,3},{3,4},{4,5},{5,6},{6,7},{7,8},{8,9},{9,10},{10,1... | collective-permute-start | bytes 49160 | tf_op jit(solution)/shard_map/ppermute | solution.py:154
